TPU v7x, 32 devices: a whole 2x2x4 slice. The times are simulated.
32 devices in a mesh: band: 8 (over z, x), dir: 4 (over y, core).
Axes of the slice: x: 2, y: 2, z: 4, core: 2. Of those that a mesh axis runs over, the one named last changes fastest.
Arguments:
- visibilities: bfloat16 [16, 32, 2, 256, 256], P('band', 'dir'), as said below
- sky_model: bfloat16 [16, 32, 2, 256, 256], P('band', 'dir')
- rfi_flags: int32 [16, 8, 8], P('band'), may hold values from 0 to 1, as said below
- destination: int32 [16], P('band'), may hold values from 0 to 15, as said below
Outputs:
- delivered: float32 [16, 32, 2, 256], P('band', 'dir')
- coefficients: float32 [9, 32, 2, 256], P(None, 'dir')
- norm_values: float32 [2, 2], replicated
Inputs may be any that keep to these rules, and one draw needn't show every extreme that they name: `rfi_flags`: 1 marks a flagged baseline block; the share of flagged blocks tends to fall with the subband index. destination holds every row of 0 to 15 once. With the rows split into 8 aligned blocks of 2 rows, one row of block i goes to a row of block i + 1 and the other to a row of block i + 4, modulo 16 // 2. `visibilities`: visibilities follow the model under unknown station gains, with noise.
All inputs are finite; a program needn't handle non-finite values.
Results may differ from a plain program's by a relative error of at most 0.0003.
Values sent between devices are 32-bit elements; how exact they have to be, the bound alone decides.
A program may use at most 128 MiB of HBM per device.

v0:
```python
import functools

import jax
import jax.numpy as jnp
from jax import lax
from jax.experimental import pallas as pl
from jax.experimental.pallas import tpu as pltpu
from jax.sharding import PartitionSpec as P

BLOCK = 32
DEGREE = 8
SWEEPS = 4
ITERS = 2
TERMS = DEGREE + 1
ROWS = 16
LANES = 128

penalty_share = 0.4
f32 = jnp.float32
bf16 = jnp.bfloat16
MESH = pl.DeviceIdType.MESH


def row_of(shape, axis=0):
    return lax.broadcasted_iota(jnp.int32, shape, axis)


def spread(value, shape):
    return jnp.broadcast_to(value, shape)


def left_side(gain):
    row = row_of(gain.shape)
    part = lax.rem(row, 4)
    re = spread(gain[0:1], gain.shape)
    im = spread(gain[1:2], gain.shape)
    zero = jnp.zeros_like(gain)
    first = jnp.where(part == 0, re, jnp.where(part == 1, im, zero))
    second = jnp.where(part == 0, -im, jnp.where(part == 1, re, zero))
    third = jnp.where(part == 2, re * re + im * im, zero)
    sides = []
    for full in (first, second, third):
        lead = full.astype(bf16).astype(f32)
        sides.append(jnp.where(row < 4, lead, full - lead).astype(bf16))
    return jnp.concatenate(sides + sides, axis=1)


def kernel(
    bands,
    dirs,
    vis_hbm,
    sky_hbm,
    flags,
    dest,
    delivered,
    coef,
    norms,
    vis,
    sky,
    oper,
    turned,
    keep,
    wpen,
    meta,
    gains,
    zall,
    uall,
    gtile,
    ttile,
    solve_rows,
    cheb_rows,
    norm_all,
    vis_sem,
    sky_sem,
    meta_send,
    meta_recv,
    gain_send,
    gain_recv,
    norm_send,
    norm_recv,
):
    subs, count, _, stations, _ = vis_hbm.shape
    blocks = flags.shape[-1]
    total = bands * subs
    width = meta.shape[-1]
    me = lax.axis_index("band")
    my_dir = lax.axis_index("dir")
    tile = (8, stations)

    def ahead(distance):
        return lax.rem(me + distance, bands)

    def behind(distance):
        return lax.rem(me + bands - distance, bands)

    def load(pair):
        s, k = divmod(pair, count)
        return (
            pltpu.make_async_copy(vis_hbm.at[s, k], vis.at[pair], vis_sem.at[pair]),
            pltpu.make_async_copy(sky_hbm.at[s, k], sky.at[pair], sky_sem.at[pair]),
        )

    for pair in range(subs * count):
        for copy in load(pair):
            copy.start()

    barrier = pltpu.get_barrier_semaphore()
    for distance in range(1, bands):
        pl.semaphore_signal(
            barrier, inc=1, device_id={"band": ahead(distance)}, device_id_type=MESH
        )
    for distance in range(1, dirs):
        pl.semaphore_signal(
            barrier,
            inc=1,
            device_id={"dir": lax.rem(my_dir + distance, dirs)},
            device_id_type=MESH,
        )

    lane_w = row_of((1, width), 1)
    weight_row = jnp.zeros((1, width), f32)
    dest_rows = []
    for s in range(subs):
        kept = (1 - flags[s]).astype(f32)
        weight = (1.0 + jnp.sum(kept, axis=(0, 1), keepdims=True)) / (1.0 + blocks * blocks)
        wpen[s] = spread(penalty_share * stations * weight, tile)
        weight_row = jnp.where(lane_w == me * subs + s, weight, weight_row)
        dest_rows.append(jnp.full((1, width), dest[s], jnp.int32).astype(f32))
        lane = row_of((1, stations), 1) // BLOCK
        for i in range(blocks):
            shape = (BLOCK, stations)
            across = jnp.zeros((1, stations), f32)
            for j in range(blocks):
                across = jnp.where(lane == j, kept[j : j + 1, i : i + 1], across)
            apart = row_of(shape) + i * BLOCK != row_of(shape, 1)
            keep[s, i * BLOCK : (i + 1) * BLOCK, :] = jnp.where(
                apart, spread(across, shape), 0.0
            )
    meta[me] = jnp.zeros(meta.shape[1:], f32)
    for s in range(subs):
        meta[me, s : s + 1, :] = dest_rows[s]
    meta[me, subs : subs + 1, :] = weight_row

    row = row_of(tile)
    for pair in range(subs * count):
        ttile[pair] = jnp.where(row == 0, 1.0, jnp.zeros(tile, f32))

    pl.semaphore_wait(barrier, bands - 1 + dirs - 1)

    def meta_copy(slot, distance):
        return pltpu.make_async_remote_copy(
            src_ref=meta.at[slot],
            dst_ref=meta.at[slot],
            send_sem=meta_send.at[distance],
            recv_sem=meta_recv.at[distance],
            device_id={"band": ahead(distance)},
            device_id_type=MESH,
        )

    def gain_copy(it, slot, s, distance):
        return pltpu.make_async_remote_copy(
            src_ref=gains.at[it, slot, s],
            dst_ref=gains.at[it, slot, s],
            send_sem=gain_send.at[it, s, distance],
            recv_sem=gain_recv.at[it, s, distance],
            device_id={"band": ahead(distance)},
            device_id_type=MESH,
        )

    def norm_copy(slot, distance):
        return pltpu.make_async_remote_copy(
            src_ref=norm_all.at[slot],
            dst_ref=norm_all.at[slot],
            send_sem=norm_send.at[distance],
            recv_sem=norm_recv.at[distance],
            device_id={"dir": lax.rem(my_dir + distance, dirs)},
            device_id_type=MESH,
        )

    for distance in range(1, bands):
        meta_copy(me, distance).start()

    square = (stations, stations)
    identity = (row_of(square) == row_of(square, 1)).astype(f32).astype(bf16)

    def build(s):
        def one(k, carry):
            pair = s * count + k
            pltpu.make_async_copy(vis_hbm.at[s, k], vis.at[pair], vis_sem.at[pair]).wait()
            pltpu.make_async_copy(sky_hbm.at[s, k], sky.at[pair], sky_sem.at[pair]).wait()
            slot = lax.rem(k, 2)
            for part, source in enumerate((vis, sky)):
                for j in range(2):
                    turned[slot, 2 * part + j] = lax.dot_general(
                        identity,
                        source[pair, j],
                        (((1,), (1,)), ((), ())),
                        preferred_element_type=f32,
                    )
            sums = [jnp.zeros(tile, f32) for _ in range(3)]
            for i in range(stations // BLOCK):
                rows = slice(i * BLOCK, (i + 1) * BLOCK)
                baseline = keep[s, rows, :]
                data_re = turned[slot, 0, rows, :]
                data_im = turned[slot, 1, rows, :]
                model_re = turned[slot, 2, rows, :]
                model_im = turned[slot, 3, rows, :]
                parts = (
                    baseline * (model_re * data_re + model_im * data_im),
                    baseline * (model_re * data_im - model_im * data_re),
                    baseline * (model_re * model_re + model_im * model_im),
                )
                for j, full in enumerate(parts):
                    for r in range(0, BLOCK, 8):
                        sums[j] = sums[j] + full[r : r + 8]
                    lead = full.astype(bf16)
                    base = j * stations + i * BLOCK
                    oper[pair, base : base + BLOCK, :] = lead
                    base = base + 3 * stations
                    oper[pair, base : base + BLOCK, :] = (full - lead.astype(f32)).astype(bf16)
            re, im, mag = (spread(jnp.sum(x, axis=0, keepdims=True), tile) for x in sums)
            out = jnp.where(row == 0, re, jnp.where(row == 1, im, 0.0))
            penalty = wpen[s]
            gtile[pair] = (out + penalty * ttile[pair]) / (mag + penalty)
            return carry

        lax.fori_loop(0, count, one, 0, unroll=2)

    def sweeps(it, s):
        penalty = wpen[s]

        def one(index, held):
            step = jnp.where(lax.rem(index, 2) == 1, 0.5, 1.0).astype(f32)
            fresh = []
            for k in range(count):
                pair = s * count + k
                gain = held[k]
                out = lax.dot_general(
                    left_side(gain),
                    oper[pair],
                    (((1,), (0,)), ((), ())),
                    preferred_element_type=f32,
                )
                out = out + pltpu.roll(out, 4, 0)
                updated = (out + penalty * ttile[pair]) / (spread(out[2:3], tile) + penalty)
                fresh.append(step * updated + (1.0 - step) * gain)
            return tuple(fresh)

        start = tuple(gtile[s * count + k] for k in range(count))
        final = lax.fori_loop(1 if it == 0 else 0, SWEEPS, one, start)
        for k in range(count):
            gtile[s * count + k] = final[k]
            gains[it, me, s, k : k + 1, 0:stations] = final[k][0:1]
            gains[it, me, s, k : k + 1, stations : 2 * stations] = final[k][1:2]

    def solve():
        weights = meta[0, subs : subs + 1, :]
        for i in range(1, bands):
            weights = weights + meta[i, subs : subs + 1, :]
        index = row_of((1, width), 1).astype(f32)
        abscissa = (2.0 * index + 1.0) / total - 1.0
        terms = [jnp.ones_like(abscissa), abscissa]
        for degree in range(2, DEGREE + 1):
            terms.append(2.0 * abscissa * terms[-1] - terms[-2])
        shape = (ROWS, width)
        cheb = jnp.zeros(shape, f32)
        for c in range(TERMS):
            cheb = jnp.where(row_of(shape) == c, spread(terms[c], shape), cheb)
        right = cheb * weights
        gram = jnp.zeros((ROWS, LANES), f32)
        for c in range(TERMS):
            column = jnp.sum(right * terms[c], axis=1, keepdims=True)
            gram = jnp.where(row_of(gram.shape, 1) == c, column, gram)
        for c in range(TERMS):
            pivot = gram[c : c + 1, c : c + 1]
            gram_row = gram[c : c + 1, :] / pivot
            right_row = right[c : c + 1, :] / pivot
            column = gram[:, c : c + 1]
            gram = jnp.where(row_of(gram.shape) == c, gram_row, gram - column * gram_row)
            right = jnp.where(row_of(shape) == c, right_row, right - column * right_row)
        cheb = jnp.where(row_of(shape) == ROWS - 1, spread(weights, shape), cheb)
        for f in range(total):
            solve_rows[f] = spread(right[:, f : f + 1], (ROWS, stations))
            cheb_rows[f] = spread(cheb[:, f : f + 1], (ROWS, stations))
        return jnp.sum(weights, axis=1, keepdims=True)

    def consensus(it):
        block = (count, stations)
        sums = []
        for half in range(2):
            lanes = slice(half * stations, (half + 1) * stations)

            def project(i, acc):
                for s in range(subs):
                    value = gains[it, i, s, :, lanes]
                    if it > 0:
                        value = value + uall[i, s, :, lanes]
                    f = i * subs + s
                    acc = tuple(
                        acc[c] + spread(solve_rows[f, c : c + 1, :], block) * value
                        for c in range(TERMS)
                    )
                return acc

            coefs = lax.fori_loop(
                0, bands, project, tuple(jnp.zeros(block, f32) for _ in range(TERMS))
            )
            if it == ITERS - 1:
                for c in range(TERMS):
                    for k in range(count):
                        coef[c, k, half : half + 1, :] = coefs[c][k : k + 1]

            def expand(i, acc):
                primal, dual = acc
                for s in range(subs):
                    f = i * subs + s
                    fresh = spread(cheb_rows[f, 0:1, :], block) * coefs[0]
                    for c in range(1, TERMS):
                        fresh = fresh + spread(cheb_rows[f, c : c + 1, :], block) * coefs[c]
                    weight = spread(cheb_rows[f, ROWS - 1 : ROWS, :], block)
                    gap = gains[it, i, s, :, lanes] - fresh
                    if it > 0:
                        moved = fresh - zall[i, s, :, lanes]
                    else:
                        moved = fresh - (1.0 - half)
                    primal = primal + weight * (gap * gap)
                    dual = dual + weight * (moved * moved)
                    if it < ITERS - 1:
                        if it > 0:
                            uall[i, s, :, lanes] = uall[i, s, :, lanes] + gap
                        else:
                            uall[i, s, :, lanes] = gap
                        zall[i, s, :, lanes] = fresh
                return primal, dual

            zero = jnp.zeros(block, f32)
            sums.append(lax.fori_loop(0, bands, expand, (zero, zero)))
        return [
            jnp.sum(sums[0][j] + sums[1][j], axis=(0, 1), keepdims=True) for j in range(2)
        ]

    norm_tile = jnp.zeros((8, LANES), f32)
    weight_sum = None
    for it in range(ITERS):
        for s in range(subs):
            if it == 0:
                build(s)
            sweeps(it, s)
            for distance in range(1, bands):
                gain_copy(it, me, s, distance).start()
        if it == 0:
            for distance in range(1, bands):
                meta_copy(behind(distance), distance).wait_recv()
            weight_sum = solve()
        for s in range(subs):
            for distance in range(1, bands):
                gain_copy(it, behind(distance), s, distance).wait_recv()
        parts = consensus(it)
        for j in range(2):
            norm_tile = jnp.where(
                (row_of(norm_tile.shape) == it) & (row_of(norm_tile.shape, 1) == j),
                parts[j],
                norm_tile,
            )
        if it < ITERS - 1:
            for s in range(subs):
                target = zall[me, s] - uall[me, s]
                for k in range(count):
                    re = spread(target[k : k + 1, 0:stations], tile)
                    im = spread(target[k : k + 1, stations : 2 * stations], tile)
                    ttile[s * count + k] = jnp.where(
                        row == 0, re, jnp.where(row == 1, im, 0.0)
                    )

    norm_all[my_dir] = norm_tile
    for distance in range(1, dirs):
        norm_copy(my_dir, distance).start()

    for s in range(subs):
        wanted = (me * subs + s).astype(f32)
        block = jnp.zeros((count, 2 * stations), f32)
        for distance in sorted({1, bands // 2}):
            source = behind(distance)
            for r in range(subs):
                here = (meta[source, r : r + 1, 0:LANES] == wanted).astype(f32)
                here = spread(here[:, 0:1], block.shape)
                block = block + here * gains[ITERS - 1, source, r]
        for k in range(count):
            delivered[s, k, 0:1, :] = block[k : k + 1, 0:stations]
            delivered[s, k, 1:2, :] = block[k : k + 1, stations : 2 * stations]

    for distance in range(1, dirs):
        norm_copy(lax.rem(my_dir + dirs - distance, dirs), distance).wait_recv()
    sum_tile = norm_all[0]
    for i in range(1, dirs):
        sum_tile = sum_tile + norm_all[i]
    final = jnp.sqrt(sum_tile / (count * dirs * 2.0 * stations * weight_sum))
    norms[...] = final[0:ITERS, 0:2]

    for distance in range(1, dirs):
        norm_copy(my_dir, distance).wait_send()
    for distance in range(1, bands):
        meta_copy(me, distance).wait_send()
        for it in range(ITERS):
            for s in range(subs):
                gain_copy(it, me, s, distance).wait_send()


def per_device(bands, dirs, visibilities, sky_model, rfi_flags, destination):
    subs, count, _, stations, _ = visibilities.shape
    pairs = subs * count
    total = bands * subs
    width = -(-total // LANES) * LANES
    meta_rows = -(-(subs + 1) // 8) * 8
    vmem = pl.BlockSpec(memory_space=pltpu.VMEM)
    hbm = pl.BlockSpec(memory_space=pl.ANY)
    sem = pltpu.SemaphoreType.DMA
    delivered, coefficients, norms = pl.pallas_call(
        functools.partial(kernel, bands, dirs),
        out_shape=(
            jax.ShapeDtypeStruct((subs, count, 2, stations), f32),
            jax.ShapeDtypeStruct((TERMS, count, 2, stations), f32),
            jax.ShapeDtypeStruct((ITERS, 2), f32),
        ),
        in_specs=[hbm, hbm, vmem, pl.BlockSpec(memory_space=pltpu.SMEM)],
        out_specs=(vmem, vmem, vmem),
        scratch_shapes=[
            pltpu.VMEM((pairs, 2, stations, stations), bf16),
            pltpu.VMEM((pairs, 2, stations, stations), bf16),
            pltpu.VMEM((pairs, 6 * stations, stations), bf16),
            pltpu.VMEM((2, 4, stations, stations), f32),
            pltpu.VMEM((subs, stations, stations), f32),
            pltpu.VMEM((subs, 8, stations), f32),
            pltpu.VMEM((bands, meta_rows, width), f32),
            pltpu.VMEM((ITERS, bands, subs, count, 2 * stations), f32),
            pltpu.VMEM((bands, subs, count, 2 * stations), f32),
            pltpu.VMEM((bands, subs, count, 2 * stations), f32),
            pltpu.VMEM((pairs, 8, stations), f32),
            pltpu.VMEM((pairs, 8, stations), f32),
            pltpu.VMEM((total, ROWS, stations), f32),
            pltpu.VMEM((total, ROWS, stations), f32),
            pltpu.VMEM((dirs, 8, LANES), f32),
            sem((pairs,)),
            sem((pairs,)),
            sem((bands,)),
            sem((bands,)),
            sem((ITERS, subs, bands)),
            sem((ITERS, subs, bands)),
            sem((dirs,)),
            sem((dirs,)),
        ],
        compiler_params=pltpu.CompilerParams(
            collective_id=0, has_side_effects=True, vmem_limit_bytes=56 * 1024 * 1024
        ),
    )(visibilities, sky_model, rfi_flags, destination)
    return delivered, coefficients, norms


def solution(mesh):
    return jax.shard_map(
        functools.partial(per_device, mesh.shape["band"], mesh.shape["dir"]),
        mesh=mesh,
        in_specs=(
            P("band", "dir", None, None, None),
            P("band", "dir", None, None, None),
            P("band", None, None),
            P("band"),
        ),
        out_specs=(P("band", "dir", None, None), P(None, "dir", None, None), P()),
        check_vma=False,
    )
```

profile of v0, /device:TPU:0, one launch (start us, length us, event | category | flops | bytes accessed | tf_op | source)
XLA Modules:
  0.0 48.9 jit_solution(8796542611864796334)
XLA Ops:
  0.6 44.1 %shard_map.67 = (f32[2,8,2,256]{3,2,1,0:T(2,128)}, f32[9,8,2,256]{3,2,1,0:T(2,128)}, f32[2,2]{1,0:T(2,128)}) custom-call(bf16[2,8,2,256,256]{4,3,2,1,0:T(8,128)(2,1)} %vis_hbm.1, bf16[2,8,2,256,256]{4,3,2,1,0:T(8,128)(2,1)} %sky_hbm.1, s32[2,8,8]{2,1,0:T(8,128)} %flags.1, s32[2]{0:T(128)} %dest.1), custom_call_target="tpu_custom_call" | custom-call | tf_op jit(solution)/shard_map/pallas_call | solution.py:418
  44.8 1.4 %copy.10 = f32[2,8,2,256]{3,2,1,0:T(2,128)} copy(f32[2,8,2,256]{3,2,1,0:T(2,128)} %get-tuple-element.6) | data formatting | bytes 65536
  46.1 1.6 %copy.11 = f32[9,8,2,256]{3,2,1,0:T(2,128)} copy(f32[9,8,2,256]{3,2,1,0:T(2,128)} %get-tuple-element.7) | data formatting | bytes 294912
  47.7 1.2 %copy.12 = f32[2,2]{1,0:T(2,128)} copy(f32[2,2]{1,0:T(2,128)} %get-tuple-element.8) | data formatting | bytes 32
where the time goes:
time: 49.2 us; the launch traced here: 48.9 us
  Pallas kernels  44.1 us (90%)
  local copies, waits for them, and re-layouts  4.18 us (8%)
  between operations  0.64 us (1%)
    pallas_call x1, Pallas kernels, per_device(): pl.pallas_call(functools.partial(kernel, bands, dirs), out_shape=(jax.Sha...  44.1 us
    unnamed x3, local copies, waits for them, and re-layouts  4.18 us

commit v1 on v0

v1 whole, which is shorter than its diff:
```python
import functools

import jax
import jax.numpy as jnp
from jax import lax
from jax.experimental import pallas as pl
from jax.experimental.pallas import tpu as pltpu
from jax.sharding import PartitionSpec as P

BLOCK = 32
DEGREE = 8
SWEEPS = 4
ITERS = 2
TERMS = DEGREE + 1
ROWS = 16
LANES = 128
TILE = 8
PLAN = (("exact", "lead", "both", "held"), ("held", "held", "both", "held"))

penalty_share = 0.4
f32 = jnp.float32
bf16 = jnp.bfloat16
MESH = pl.DeviceIdType.MESH


def row_of(shape, axis=0):
    return lax.broadcasted_iota(jnp.int32, shape, axis)


def spread(value, shape):
    return jnp.broadcast_to(value, shape)


def repeat(count, body, carry):
    if count <= 8:
        for i in range(count):
            carry = body(i, carry)
        return carry
    return lax.fori_loop(0, count, body, carry)


def kernel(
    bands,
    dirs,
    group,
    vis_hbm,
    sky_hbm,
    flags,
    dest,
    delivered,
    coef,
    norms,
    vis,
    sky,
    lead_num,
    lead_den,
    rest_num,
    rest_den,
    turned,
    keep,
    wpen,
    meta,
    gains,
    zall,
    uall,
    held,
    solve_rows,
    cheb_rows,
    solve_tiles,
    cheb_tiles,
    norm_all,
    vis_sem,
    sky_sem,
    meta_send,
    meta_recv,
    gain_send,
    gain_recv,
    norm_send,
    norm_recv,
):
    subs, count, _, stations, _ = vis_hbm.shape
    blocks = flags.shape[-1]
    total = bands * subs
    width = meta.shape[-1]
    chunks = count // group
    pairs = subs * group
    rows = 2 * pairs
    me = lax.axis_index("band")
    my_dir = lax.axis_index("dir")
    tile = (rows, stations)

    def ahead(distance):
        return lax.rem(me + distance, bands)

    def behind(distance):
        return lax.rem(me + bands - distance, bands)

    def load(c, j):
        s, k = j // group, c * group + j % group
        slot = c * pairs + j
        return (
            pltpu.make_async_copy(vis_hbm.at[s, k], vis.at[slot], vis_sem.at[slot]),
            pltpu.make_async_copy(sky_hbm.at[s, k], sky.at[slot], sky_sem.at[slot]),
        )

    for c in range(chunks):
        for j in range(pairs):
            for copy in load(c, j):
                copy.start()

    barrier = pltpu.get_barrier_semaphore()
    for distance in range(1, bands):
        pl.semaphore_signal(
            barrier, inc=1, device_id={"band": ahead(distance)}, device_id_type=MESH
        )
    for distance in range(1, dirs):
        pl.semaphore_signal(
            barrier,
            inc=1,
            device_id={"dir": lax.rem(my_dir + distance, dirs)},
            device_id_type=MESH,
        )

    row = row_of(tile)
    odd = lax.rem(row, 2) == 1
    sub_row = row // (2 * group)

    lane_w = row_of((1, width), 1)
    weight_row = jnp.zeros((1, width), f32)
    penalty = jnp.zeros(tile, f32)
    dest_rows = []
    for s in range(subs):
        kept = (1 - flags[s]).astype(f32)
        weight = (1.0 + jnp.sum(kept, axis=(0, 1), keepdims=True)) / (1.0 + blocks * blocks)
        penalty = jnp.where(sub_row == s, spread(penalty_share * stations * weight, tile), penalty)
        weight_row = jnp.where(lane_w == me * subs + s, weight, weight_row)
        dest_rows.append(jnp.full((1, width), dest[s], jnp.int32).astype(f32))
        lane = row_of((1, stations), 1) // BLOCK
        for i in range(blocks):
            shape = (BLOCK, stations)
            across = jnp.zeros((1, stations), f32)
            for j in range(blocks):
                across = jnp.where(lane == j, kept[j : j + 1, i : i + 1], across)
            apart = row_of(shape) + i * BLOCK != row_of(shape, 1)
            keep[s, i * BLOCK : (i + 1) * BLOCK, :] = jnp.where(
                apart, spread(across, shape), 0.0
            )
    wpen[...] = penalty
    meta[me] = jnp.zeros(meta.shape[1:], f32)
    for s in range(subs):
        meta[me, s : s + 1, :] = dest_rows[s]
    meta[me, subs : subs + 1, :] = weight_row

    def meta_copy(slot, distance):
        return pltpu.make_async_remote_copy(
            src_ref=meta.at[slot],
            dst_ref=meta.at[slot],
            send_sem=meta_send.at[distance],
            recv_sem=meta_recv.at[distance],
            device_id={"band": ahead(distance)},
            device_id_type=MESH,
        )

    def gain_copy(it, c, slot, distance):
        return pltpu.make_async_remote_copy(
            src_ref=gains.at[it, c, slot],
            dst_ref=gains.at[it, c, slot],
            send_sem=gain_send.at[it, c, distance],
            recv_sem=gain_recv.at[it, c, distance],
            device_id={"band": ahead(distance)},
            device_id_type=MESH,
        )

    def norm_copy(slot, distance):
        return pltpu.make_async_remote_copy(
            src_ref=norm_all.at[slot],
            dst_ref=norm_all.at[slot],
            send_sem=norm_send.at[distance],
            recv_sem=norm_recv.at[distance],
            device_id={"dir": lax.rem(my_dir + distance, dirs)},
            device_id_type=MESH,
        )

    square = (stations, stations)
    identity = (row_of(square) == row_of(square, 1)).astype(f32).astype(bf16)
    ones = jnp.where(odd, jnp.zeros(tile, f32), 1.0)

    def swapped(value):
        return jnp.where(odd, pltpu.roll(value, 1, 0), pltpu.roll(value, rows - 1, 0))

    pick_row = row_of((2 * rows, stations))
    pick_pair = lax.rem(pick_row, rows) // 2
    picks = [
        jnp.where(pick_pair == j, jnp.ones(pick_row.shape, f32), 0.0).astype(bf16)
        for j in range(pairs)
    ]

    def left_sides(gain):
        other = swapped(gain)
        sides = []
        for full in (gain, jnp.where(odd, other, -other), gain * gain + other * other):
            lead = full.astype(bf16).astype(f32)
            sides.append(jnp.concatenate([lead, full - lead], axis=0).astype(bf16))
        num, den = [], []
        for j in range(pairs):
            num += [sides[0] * picks[j], sides[1] * picks[j]]
            den.append(sides[2] * picks[j])
        return jnp.concatenate(num, axis=1), jnp.concatenate(den, axis=1)

    def times(left, right):
        out = lax.dot_general(
            left, right, (((1,), (0,)), ((), ())), preferred_element_type=f32
        )
        return out[:rows] + out[rows:]

    def solved(num, den, target):
        pen = wpen[...]
        return (num + pen * target) / (den + pen)

    def build(c, out):
        num = jnp.zeros(tile, f32)
        den = jnp.zeros(tile, f32)

        def turn(j):
            slot = c * pairs + j
            for part, source in enumerate((vis, sky)):
                for i in range(2):
                    turned[j, 2 * part + i] = lax.dot_general(
                        identity,
                        source[slot, i],
                        (((1,), (1,)), ((), ())),
                        preferred_element_type=f32,
                    )

        def fill(j, num, den):
            s = j // group
            sums = [jnp.zeros((TILE, stations), f32) for _ in range(3)]
            for i in range(stations // BLOCK):
                part = slice(i * BLOCK, (i + 1) * BLOCK)
                baseline = keep[s, part, :]
                data_re = turned[j, 0, part, :]
                data_im = turned[j, 1, part, :]
                model_re = baseline * turned[j, 2, part, :]
                model_im = baseline * turned[j, 3, part, :]
                values = (
                    model_re * data_re + model_im * data_im,
                    model_re * data_im - model_im * data_re,
                    model_re * model_re + model_im * model_im,
                )
                for n, full in enumerate(values):
                    for r in range(0, BLOCK, TILE):
                        sums[n] = sums[n] + full[r : r + TILE]
                    lead = full.astype(bf16)
                    rest = (full - lead.astype(f32)).astype(bf16)
                    if n < 2:
                        base = (2 * j + n) * stations + i * BLOCK
                        lead_num[c, base : base + BLOCK, :] = lead
                        rest_num[c, base : base + BLOCK, :] = rest
                    else:
                        base = j * stations + i * BLOCK
                        lead_den[c, base : base + BLOCK, :] = lead
                        rest_den[c, base : base + BLOCK, :] = rest
            re, im, mag = (spread(jnp.sum(x, axis=0, keepdims=True), tile) for x in sums)
            num = jnp.where(row == 2 * j, re, jnp.where(row == 2 * j + 1, im, num))
            den = jnp.where(row // 2 == j, mag, den)
            return num, den

        for j in range(pairs):
            turn(j)
            num, den = fill(j, num, den)
            yield
        out[c] = solved(num, den, ones)

    def sweeps(it, c, gain, out):
        target = ones if it == 0 else zall[c, me] - uall[c, me]
        for index in range(SWEEPS):
            mode = PLAN[it][index]
            if mode == "exact":
                continue
            left_num, left_den = left_sides(gain)
            num = times(left_num, lead_num[c])
            den = times(left_den, lead_den[c])
            if mode == "both":
                low_num = times(left_num, rest_num[c])
                low_den = times(left_den, rest_den[c])
                held[c, 0] = low_num
                held[c, 1] = low_den
                num, den = num + low_num, den + low_den
            yield
            if mode == "held":
                num, den = num + held[c, 0], den + held[c, 1]
            updated = solved(num, den, target)
            gain = 0.5 * (updated + gain) if index % 2 == 1 else updated
        out[c] = gain

    def together(*steps):
        steps = list(steps)
        while steps:
            for step in list(steps):
                try:
                    next(step)
                except StopIteration:
                    steps.remove(step)

    def send(it, c, gain):
        gains[it, c, me] = gain
        for distance in range(1, bands):
            gain_copy(it, c, me, distance).start()

    def arrive(it, c):
        for distance in range(1, bands):
            gain_copy(it, c, behind(distance), distance).wait_recv()

    def solve():
        weights = meta[0, subs : subs + 1, :]
        for i in range(1, bands):
            weights = weights + meta[i, subs : subs + 1, :]
        index = row_of((1, width), 1).astype(f32)
        abscissa = (2.0 * index + 1.0) / total - 1.0
        terms = [jnp.ones_like(abscissa), abscissa]
        for degree in range(2, DEGREE + 1):
            terms.append(2.0 * abscissa * terms[-1] - terms[-2])
        shape = (ROWS, width)
        cheb = jnp.zeros(shape, f32)
        for c in range(TERMS):
            cheb = jnp.where(row_of(shape) == c, spread(terms[c], shape), cheb)
        right = cheb * weights
        gram = jnp.zeros((ROWS, LANES), f32)
        for c in range(TERMS):
            column = jnp.sum(right * terms[c], axis=1, keepdims=True)
            gram = jnp.where(row_of(gram.shape, 1) == c, column, gram)
        for c in range(TERMS):
            pivot = gram[c : c + 1, c : c + 1]
            gram_row = gram[c : c + 1, :] / pivot
            right_row = right[c : c + 1, :] / pivot
            column = gram[:, c : c + 1]
            gram = jnp.where(row_of(gram.shape) == c, gram_row, gram - column * gram_row)
            right = jnp.where(row_of(shape) == c, right_row, right - column * right_row)
        cheb = jnp.where(row_of(shape) == ROWS - 1, spread(weights, shape), cheb)
        for f in range(total):
            solve_rows[f] = spread(right[:, f : f + 1], (ROWS, LANES))
            cheb_rows[f] = spread(cheb[:, f : f + 1], (ROWS, LANES))

        half = (rows, LANES)
        sub = row_of(half) // (2 * group)

        def lay(i, carry):
            for source, tiles, used in (
                (solve_rows, solve_tiles, range(TERMS)),
                (cheb_rows, cheb_tiles, [*range(TERMS), ROWS - 1]),
            ):
                for n, c in enumerate(used):
                    value = spread(source[i * subs, c : c + 1, :], half)
                    for s in range(1, subs):
                        more = spread(source[i * subs + s, c : c + 1, :], half)
                        value = jnp.where(sub == s, more, value)
                    tiles[i, n] = value
            return carry

        repeat(bands, lay, 0)
        return jnp.sum(weights, axis=1, keepdims=True)

    def consensus(it, c, sums):
        parts = [slice(at, at + LANES) for at in range(0, stations, LANES)]
        zero = jnp.zeros((rows, LANES), f32)
        lanes = len(parts)

        def project(i, acc):
            values = []
            for part in parts:
                value = gains[it, c, i, :, part]
                if it > 0:
                    value = value + uall[c, i, :, part]
                values.append(value)
            acc = list(acc)
            for n in range(TERMS):
                scale = solve_tiles[i, n]
                for h in range(lanes):
                    acc[n * lanes + h] = acc[n * lanes + h] + scale * values[h]
            return tuple(acc)

        acc = repeat(bands, project, (zero,) * (TERMS * lanes))
        coefs = []
        for one in acc:
            value = one
            for s in range(1, subs):
                value = value + pltpu.roll(one, s * 2 * group, 0)
            coefs.append(value)
        if it == ITERS - 1:
            for n in range(TERMS):
                for h, part in enumerate(parts):
                    for k in range(group):
                        coef[n, c * group + k, :, part] = coefs[n * lanes + h][2 * k : 2 * k + 2]
        unit = jnp.where(lax.rem(row_of(zero.shape), 2) == 1, zero, 1.0)

        def expand(i, sums):
            primal, dual = sums
            scales = [cheb_tiles[i, n] for n in range(TERMS + 1)]
            for h, part in enumerate(parts):
                fresh = scales[0] * coefs[h]
                for n in range(1, TERMS):
                    fresh = fresh + scales[n] * coefs[n * lanes + h]
                gap = gains[it, c, i, :, part] - fresh
                moved = fresh - (zall[c, i, :, part] if it > 0 else unit)
                primal = primal + scales[TERMS] * (gap * gap)
                dual = dual + scales[TERMS] * (moved * moved)
                if it < ITERS - 1:
                    uall[c, i, :, part] = uall[c, i, :, part] + gap if it > 0 else gap
                    zall[c, i, :, part] = fresh
            return primal, dual

        return repeat(bands, expand, sums)

    def deliver(c, marks):
        block = jnp.zeros(tile, f32)
        for n, distance in enumerate(sorted({1, bands // 2})):
            source = gains[ITERS - 1, c, behind(distance)]
            for turn in range(subs):
                moved = pltpu.roll(source, turn * 2 * group, 0) if turn else source
                block = block + marks[n][turn] * moved
        for s in range(subs):
            for k in range(group):
                base = 2 * (s * group + k)
                delivered[s, c * group + k] = block[base : base + 2]

    first, after = {}, {}
    for c in range(chunks):
        for j in range(pairs):
            for copy in load(c, j):
                copy.wait()
        if c == 1:
            pl.semaphore_wait(barrier, bands - 1 + dirs - 1)
            for distance in range(1, bands):
                meta_copy(me, distance).start()
        steps = [build(c, first)]
        if c > 0:
            steps.insert(0, sweeps(0, c - 1, first[c - 1], after))
        together(*steps)
        if c > 0:
            send(0, c - 1, after[c - 1])
    for distance in range(1, bands):
        meta_copy(behind(distance), distance).wait_recv()
    together(sweeps(0, chunks - 1, first[chunks - 1], after))
    send(0, chunks - 1, after[chunks - 1])
    weight_sum = solve()

    zero = jnp.zeros((rows, LANES), f32)
    totals = [(zero, zero) for _ in range(ITERS)]
    pace = 2 if chunks % 2 == 0 else 1
    for base in range(0, chunks, pace):
        here = range(base, base + pace)
        for c in here:
            arrive(0, c)
            totals[0] = consensus(0, c, totals[0])
        together(*(sweeps(1, c, gains[0, c, me], after) for c in here))
        for c in here:
            send(1, c, after[c])

    marks = []
    lane_rows = (rows, LANES)
    for distance in sorted({1, bands // 2}):
        source = behind(distance)
        by_turn = []
        for turn in range(subs):
            mark = jnp.zeros(tile, f32)
            for s in range(subs):
                wanted = (me * subs + s).astype(f32)
                r = (s - turn) % subs
                here = (meta[source, r : r + 1, 0:LANES] == wanted).astype(f32)
                mark = jnp.where(sub_row == s, spread(here[:, 0:1], tile), mark)
            by_turn.append(mark)
        marks.append(by_turn)
    for c in range(chunks):
        arrive(1, c)
        totals[1] = consensus(1, c, totals[1])
        deliver(c, marks)

    norm_tile = jnp.zeros((TILE, LANES), f32)
    for it in range(ITERS):
        for j in range(2):
            norm_tile = jnp.where(
                row_of(norm_tile.shape) == 2 * it + j,
                jnp.sum(totals[it][j], axis=0, keepdims=True),
                norm_tile,
            )
    norm_all[my_dir] = norm_tile
    for distance in range(1, dirs):
        norm_copy(my_dir, distance).start()
    for distance in range(1, dirs):
        norm_copy(lax.rem(my_dir + dirs - distance, dirs), distance).wait_recv()
    sum_tile = norm_all[0]
    for i in range(1, dirs):
        sum_tile = sum_tile + norm_all[i]
    sums = jnp.sum(sum_tile, axis=1, keepdims=True)
    final = jnp.sqrt(sums / (count * dirs * 2.0 * stations * weight_sum))
    for it in range(ITERS):
        for j in range(2):
            norms[it : it + 1, j : j + 1] = final[2 * it + j : 2 * it + j + 1]

    for distance in range(1, dirs):
        norm_copy(my_dir, distance).wait_send()
    for distance in range(1, bands):
        meta_copy(me, distance).wait_send()
        for it in range(ITERS):
            for c in range(chunks):
                gain_copy(it, c, me, distance).wait_send()


def per_device(bands, dirs, visibilities, sky_model, rfi_flags, destination):
    subs, count, _, stations, _ = visibilities.shape
    total = bands * subs
    width = -(-total // LANES) * LANES
    meta_rows = -(-(subs + 1) // 8) * 8
    group = max(1, TILE // (2 * subs))
    chunks = count // group
    pairs = subs * group
    rows = 2 * pairs
    vmem = pl.BlockSpec(memory_space=pltpu.VMEM)
    hbm = pl.BlockSpec(memory_space=pl.ANY)
    sem = pltpu.SemaphoreType.DMA
    delivered, coefficients, norms = pl.pallas_call(
        functools.partial(kernel, bands, dirs, group),
        out_shape=(
            pltpu.VMEM((subs, count, 2, stations), f32),
            pltpu.VMEM((TERMS, count, 2, stations), f32),
            pltpu.VMEM((ITERS, 2), f32),
        ),
        in_specs=[hbm, hbm, vmem, pl.BlockSpec(memory_space=pltpu.SMEM)],
        out_specs=(vmem, vmem, vmem),
        scratch_shapes=[
            pltpu.VMEM((subs * count, 2, stations, stations), bf16),
            pltpu.VMEM((subs * count, 2, stations, stations), bf16),
            pltpu.VMEM((chunks, 2 * pairs * stations, stations), bf16),
            pltpu.VMEM((chunks, pairs * stations, stations), bf16),
            pltpu.VMEM((chunks, 2 * pairs * stations, stations), bf16),
            pltpu.VMEM((chunks, pairs * stations, stations), bf16),
            pltpu.VMEM((pairs, 4, stations, stations), f32),
            pltpu.VMEM((subs, stations, stations), f32),
            pltpu.VMEM((rows, stations), f32),
            pltpu.VMEM((bands, meta_rows, width), f32),
            pltpu.VMEM((ITERS, chunks, bands, rows, stations), f32),
            pltpu.VMEM((chunks, bands, rows, stations), f32),
            pltpu.VMEM((chunks, bands, rows, stations), f32),
            pltpu.VMEM((chunks, 2, rows, stations), f32),
            pltpu.VMEM((total, ROWS, LANES), f32),
            pltpu.VMEM((total, ROWS, LANES), f32),
            pltpu.VMEM((bands, TERMS, rows, LANES), f32),
            pltpu.VMEM((bands, TERMS + 1, rows, LANES), f32),
            pltpu.VMEM((dirs, TILE, LANES), f32),
            sem((subs * count,)),
            sem((subs * count,)),
            sem((bands,)),
            sem((bands,)),
            sem((ITERS, chunks, bands)),
            sem((ITERS, chunks, bands)),
            sem((dirs,)),
            sem((dirs,)),
        ],
        compiler_params=pltpu.CompilerParams(
            collective_id=0, has_side_effects=True, vmem_limit_bytes=56 * 1024 * 1024
        ),
    )(visibilities, sky_model, rfi_flags, destination)
    return delivered, coefficients, norms


def solution(mesh):
    return jax.shard_map(
        functools.partial(per_device, mesh.shape["band"], mesh.shape["dir"]),
        mesh=mesh,
        in_specs=(
            P("band", "dir", None, None, None),
            P("band", "dir", None, None, None),
            P("band", None, None),
            P("band"),
        ),
        out_specs=(P("band", "dir", None, None), P(None, "dir", None, None), P()),
        check_vma=False,
    )
```

time: 49.2 us -> 33 us (0.67)
  Pallas kernels: 44.1 us -> 30.3 us
  local copies, waits for them, and re-layouts: 4.18 us -> 1.84 us
    pallas_call x1, Pallas kernels: 44.1 us -> 30.3 us  [per_device(): pl.pallas_call(functools.partial(kernel, bands, dirs, group), out_shape=(...]
    unnamed x3, local copies, waits for them, and re-layouts: 4.18 us -> 1.84 us
where the time goes in v1:
time: 33 us; the launch traced here: 32.8 us
  Pallas kernels  30.3 us (92%)
  local copies, waits for them, and re-layouts  1.84 us (6%)
  between operations  0.64 us (2%)
    pallas_call x1, Pallas kernels, per_device(): pl.pallas_call(functools.partial(kernel, bands, dirs, group), out_shape=(...  30.3 us
    unnamed x3, local copies, waits for them, and re-layouts  1.84 us

profile of v1, /device:TPU:0, one launch (start us, length us, event | category | flops | bytes accessed | tf_op | source)
XLA Modules:
  0.0 32.8 jit_solution(17864763614141869623)
XLA Ops:
  0.6 30.3 %shard_map.67 = (f32[2,8,2,256]{3,2,1,0:T(2,128)S(1)}, f32[9,8,2,256]{3,2,1,0:T(2,128)S(1)}, f32[2,2]{1,0:T(2,128)S(1)}) custom-call(bf16[2,8,2,256,256]{4,3,2,1,0:T(8,128)(2,1)} %vis_hbm.1, bf16[2,8,2,256,256]{4,3,2,1,0:T(8,128)(2,1)} %sky_hbm.1, s32[2,8,8]{2,1,0:T(8,128)} %flags.1, s32[2]{0:T(128)} %dest.1), custom_call_target="tpu_custom_call" | custom-call | tf_op jit(solution)/shard_map/pallas_call | solution.py:521
  30.9 0.6 %copy.10 = f32[2,8,2,256]{3,2,1,0:T(2,128)} copy(f32[2,8,2,256]{3,2,1,0:T(2,128)S(1)} %get-tuple-element.3) | data formatting | bytes 65536
  31.6 0.6 %copy.12 = f32[2,2]{1,0:T(2,128)} copy(f32[2,2]{1,0:T(2,128)S(1)} %get-tuple-element.5) | data formatting | bytes 32
  32.1 0.7 %copy.11 = f32[9,8,2,256]{3,2,1,0:T(2,128)} copy(f32[9,8,2,256]{3,2,1,0:T(2,128)S(1)} %get-tuple-element.4) | data formatting | bytes 294912

commit v2 on v1

--- a/solution.py
+++ b/solution.py
@@ -45,11 +45,13 @@
     group,
     vis_hbm,
     sky_hbm,
-    flags,
-    dest,
+    flags_hbm,
+    dest_hbm,
     delivered,
     coef,
     norms,
+    flags,
+    dest,
     vis,
     sky,
     lead_num,
@@ -69,8 +71,8 @@
     solve_tiles,
     cheb_tiles,
     norm_all,
-    vis_sem,
-    sky_sem,
+    small_sem,
+    load_sem,
     meta_send,
     meta_recv,
     gain_send,
@@ -89,30 +91,41 @@
     my_dir = lax.axis_index("dir")
     tile = (rows, stations)
 
-    def ahead(distance):
-        return lax.rem(me + distance, bands)
+    def across(distance):
+        peer, bit = me, 1
+        while bit <= distance:
+            if distance // bit % 2:
+                peer = peer + bit - 2 * bit * lax.rem(me // bit, 2)
+            bit *= 2
+        return peer
+
+    if bands & (bands - 1) == 0:
+        peers = [across(distance) for distance in range(bands - 1, 0, -1)]
+    else:
+        peers = [lax.rem(me + distance, bands) for distance in range(1, bands)]
 
     def behind(distance):
         return lax.rem(me + bands - distance, bands)
 
-    def load(c, j):
-        s, k = j // group, c * group + j % group
-        slot = c * pairs + j
+    def load(c):
+        part = pl.ds(c * group, group)
         return (
-            pltpu.make_async_copy(vis_hbm.at[s, k], vis.at[slot], vis_sem.at[slot]),
-            pltpu.make_async_copy(sky_hbm.at[s, k], sky.at[slot], sky_sem.at[slot]),
+            pltpu.make_async_copy(vis_hbm.at[:, part], vis.at[c], load_sem.at[0, c]),
+            pltpu.make_async_copy(sky_hbm.at[:, part], sky.at[c], load_sem.at[1, c]),
         )
 
-    for c in range(chunks):
-        for j in range(pairs):
-            for copy in load(c, j):
-                copy.start()
+    small = (
+        pltpu.make_async_copy(flags_hbm, flags, small_sem.at[0]),
+        pltpu.make_async_copy(dest_hbm, dest, small_sem.at[1]),
+    )
+    for copy in small:
+        copy.start()
+    for copy in load(0):
+        copy.start()
 
     barrier = pltpu.get_barrier_semaphore()
-    for distance in range(1, bands):
-        pl.semaphore_signal(
-            barrier, inc=1, device_id={"band": ahead(distance)}, device_id_type=MESH
-        )
+    for peer in peers:
+        pl.semaphore_signal(barrier, inc=1, device_id={"band": peer}, device_id_type=MESH)
     for distance in range(1, dirs):
         pl.semaphore_signal(
             barrier,
@@ -121,6 +134,10 @@
             device_id_type=MESH,
         )
 
+    for copy in small:
+        copy.wait()
+    for copy in load(1) if chunks > 1 else ():
+        copy.start()
     row = row_of(tile)
     odd = lax.rem(row, 2) == 1
     sub_row = row // (2 * group)
@@ -151,23 +168,23 @@
         meta[me, s : s + 1, :] = dest_rows[s]
     meta[me, subs : subs + 1, :] = weight_row
 
-    def meta_copy(slot, distance):
+    def meta_copy(slot, peer):
         return pltpu.make_async_remote_copy(
             src_ref=meta.at[slot],
             dst_ref=meta.at[slot],
-            send_sem=meta_send.at[distance],
-            recv_sem=meta_recv.at[distance],
-            device_id={"band": ahead(distance)},
+            send_sem=meta_send,
+            recv_sem=meta_recv,
+            device_id={"band": peer},
             device_id_type=MESH,
         )
 
-    def gain_copy(it, c, slot, distance):
+    def gain_copy(it, c, slot, peer):
         return pltpu.make_async_remote_copy(
             src_ref=gains.at[it, c, slot],
             dst_ref=gains.at[it, c, slot],
-            send_sem=gain_send.at[it, c, distance],
-            recv_sem=gain_recv.at[it, c, distance],
-            device_id={"band": ahead(distance)},
+            send_sem=gain_send.at[it],
+            recv_sem=gain_recv.at[it, c],
+            device_id={"band": peer},
             device_id_type=MESH,
         )
 
@@ -175,11 +192,14 @@
         return pltpu.make_async_remote_copy(
             src_ref=norm_all.at[slot],
             dst_ref=norm_all.at[slot],
-            send_sem=norm_send.at[distance],
-            recv_sem=norm_recv.at[distance],
+            send_sem=norm_send,
+            recv_sem=norm_recv,
             device_id={"dir": lax.rem(my_dir + distance, dirs)},
             device_id_type=MESH,
         )
+
+    def all_of(ref, sem):
+        return pltpu.make_async_copy(ref, ref, sem)
 
     square = (stations, stations)
     identity = (row_of(square) == row_of(square, 1)).astype(f32).astype(bf16)
@@ -222,12 +242,11 @@
         den = jnp.zeros(tile, f32)
 
         def turn(j):
-            slot = c * pairs + j
             for part, source in enumerate((vis, sky)):
                 for i in range(2):
                     turned[j, 2 * part + i] = lax.dot_general(
                         identity,
-                        source[slot, i],
+                        source[c, j // group, j % group, i],
                         (((1,), (1,)), ((), ())),
                         preferred_element_type=f32,
                     )
@@ -304,14 +323,13 @@
 
     def send(it, c, gain):
         gains[it, c, me] = gain
-        for distance in range(1, bands):
-            gain_copy(it, c, me, distance).start()
+        for peer in peers:
+            gain_copy(it, c, me, peer).start()
 
     def arrive(it, c):
-        for distance in range(1, bands):
-            gain_copy(it, c, behind(distance), distance).wait_recv()
-
-    def solve():
+        all_of(gains.at[it, c, pl.ds(0, bands - 1)], gain_recv.at[it, c]).wait()
+
+    def solve(out):
         weights = meta[0, subs : subs + 1, :]
         for i in range(1, bands):
             weights = weights + meta[i, subs : subs + 1, :]
@@ -329,6 +347,7 @@
         for c in range(TERMS):
             column = jnp.sum(right * terms[c], axis=1, keepdims=True)
             gram = jnp.where(row_of(gram.shape, 1) == c, column, gram)
+        yield
         for c in range(TERMS):
             pivot = gram[c : c + 1, c : c + 1]
             gram_row = gram[c : c + 1, :] / pivot
@@ -336,6 +355,7 @@
             column = gram[:, c : c + 1]
             gram = jnp.where(row_of(gram.shape) == c, gram_row, gram - column * gram_row)
             right = jnp.where(row_of(shape) == c, right_row, right - column * right_row)
+        yield
         cheb = jnp.where(row_of(shape) == ROWS - 1, spread(weights, shape), cheb)
         for f in range(total):
             solve_rows[f] = spread(right[:, f : f + 1], (ROWS, LANES))
@@ -358,7 +378,7 @@
             return carry
 
         repeat(bands, lay, 0)
-        return jnp.sum(weights, axis=1, keepdims=True)
+        out["weights"] = jnp.sum(weights, axis=1, keepdims=True)
 
     def consensus(it, c, sums):
         parts = [slice(at, at + LANES) for at in range(0, stations, LANES)]
@@ -425,24 +445,25 @@
 
     first, after = {}, {}
     for c in range(chunks):
-        for j in range(pairs):
-            for copy in load(c, j):
-                copy.wait()
+        for copy in load(c):
+            copy.wait()
+        for n in range(max(2, c + 2), chunks if c == 0 else 0):
+            for copy in load(n):
+                copy.start()
         if c == 1:
             pl.semaphore_wait(barrier, bands - 1 + dirs - 1)
-            for distance in range(1, bands):
-                meta_copy(me, distance).start()
+            for peer in peers:
+                meta_copy(me, peer).start()
         steps = [build(c, first)]
         if c > 0:
             steps.insert(0, sweeps(0, c - 1, first[c - 1], after))
         together(*steps)
         if c > 0:
             send(0, c - 1, after[c - 1])
-    for distance in range(1, bands):
-        meta_copy(behind(distance), distance).wait_recv()
-    together(sweeps(0, chunks - 1, first[chunks - 1], after))
+    all_of(meta.at[pl.ds(0, bands - 1)], meta_recv).wait()
+    together(solve(after), sweeps(0, chunks - 1, first[chunks - 1], after))
     send(0, chunks - 1, after[chunks - 1])
-    weight_sum = solve()
+    weight_sum = after["weights"]
 
     zero = jnp.zeros((rows, LANES), f32)
     totals = [(zero, zero) for _ in range(ITERS)]
@@ -486,8 +507,7 @@
     norm_all[my_dir] = norm_tile
     for distance in range(1, dirs):
         norm_copy(my_dir, distance).start()
-    for distance in range(1, dirs):
-        norm_copy(lax.rem(my_dir + dirs - distance, dirs), distance).wait_recv()
+    all_of(norm_all.at[pl.ds(0, dirs - 1)], norm_recv).wait()
     sum_tile = norm_all[0]
     for i in range(1, dirs):
         sum_tile = sum_tile + norm_all[i]
@@ -497,13 +517,22 @@
         for j in range(2):
             norms[it : it + 1, j : j + 1] = final[2 * it + j : 2 * it + j + 1]
 
-    for distance in range(1, dirs):
-        norm_copy(my_dir, distance).wait_send()
-    for distance in range(1, bands):
-        meta_copy(me, distance).wait_send()
-        for it in range(ITERS):
-            for c in range(chunks):
-                gain_copy(it, c, me, distance).wait_send()
+    all_of(norm_all.at[pl.ds(0, dirs - 1)], norm_send).wait()
+    all_of(meta.at[pl.ds(0, bands - 1)], meta_send).wait()
+    for it in range(ITERS):
+        all_of(gains.at[it, :, pl.ds(0, bands - 1)], gain_send.at[it]).wait()
+
+
+def put_out(*refs):
+    count = len(refs) // 2
+    sems = refs[-1]
+    copies = [
+        pltpu.make_async_copy(refs[i], refs[count + i], sems.at[i]) for i in range(count)
+    ]
+    for copy in copies:
+        copy.start()
+    for copy in copies:
+        copy.wait()
 
 
 def per_device(bands, dirs, visibilities, sky_model, rfi_flags, destination):
@@ -525,11 +554,13 @@
             pltpu.VMEM((TERMS, count, 2, stations), f32),
             pltpu.VMEM((ITERS, 2), f32),
         ),
-        in_specs=[hbm, hbm, vmem, pl.BlockSpec(memory_space=pltpu.SMEM)],
+        in_specs=[hbm, hbm, hbm, hbm],
         out_specs=(vmem, vmem, vmem),
         scratch_shapes=[
-            pltpu.VMEM((subs * count, 2, stations, stations), bf16),
-            pltpu.VMEM((subs * count, 2, stations, stations), bf16),
+            pltpu.VMEM(rfi_flags.shape, jnp.int32),
+            pltpu.SMEM(destination.shape, jnp.int32),
+            pltpu.VMEM((chunks, subs, group, 2, stations, stations), bf16),
+            pltpu.VMEM((chunks, subs, group, 2, stations, stations), bf16),
             pltpu.VMEM((chunks, 2 * pairs * stations, stations), bf16),
             pltpu.VMEM((chunks, pairs * stations, stations), bf16),
             pltpu.VMEM((chunks, 2 * pairs * stations, stations), bf16),
@@ -547,20 +578,30 @@
             pltpu.VMEM((bands, TERMS, rows, LANES), f32),
             pltpu.VMEM((bands, TERMS + 1, rows, LANES), f32),
             pltpu.VMEM((dirs, TILE, LANES), f32),
-            sem((subs * count,)),
-            sem((subs * count,)),
-            sem((bands,)),
-            sem((bands,)),
-            sem((ITERS, chunks, bands)),
-            sem((ITERS, chunks, bands)),
-            sem((dirs,)),
-            sem((dirs,)),
+            sem((2,)),
+            sem((2, chunks)),
+            sem(()),
+            sem(()),
+            sem((ITERS,)),
+            sem((ITERS, chunks)),
+            sem(()),
+            sem(()),
         ],
         compiler_params=pltpu.CompilerParams(
             collective_id=0, has_side_effects=True, vmem_limit_bytes=56 * 1024 * 1024
         ),
     )(visibilities, sky_model, rfi_flags, destination)
-    return delivered, coefficients, norms
+    found = tuple(
+        pltpu.with_memory_space_constraint(x, pltpu.MemorySpace.VMEM)
+        for x in (delivered, coefficients, norms)
+    )
+    return pl.pallas_call(
+        put_out,
+        out_shape=tuple(jax.ShapeDtypeStruct(x.shape, x.dtype) for x in found),
+        in_specs=[vmem] * len(found),
+        out_specs=tuple([hbm] * len(found)),
+        scratch_shapes=[sem((len(found),))],
+    )(*found)
 
 
 def solution(mesh):

time: 33 us -> 29.1 us (0.88)
  Pallas kernels: 30.3 us -> 28.2 us
  local copies, waits for them, and re-layouts: 1.84 us -> 0 us
    pallas_call x1, Pallas kernels: 30.3 us -> 27.5 us  [per_device(): pl.pallas_call(functools.partial(kernel, bands, dirs, group), out_shape=(...]
    unnamed x3 -> x0, local copies, waits for them, and re-layouts: 1.84 us -> none
    pallas_call x0 -> x1, Pallas kernels: none -> 0.7 us  [per_device(): pl.pallas_call(put_out, out_shape=tuple((jax.ShapeDtypeStruct(x.shape, x....]
where the time goes in v2:
time: 29.1 us; the launch traced here: 28.9 us
  Pallas kernels  28.2 us (97%)
  between operations  0.64 us (2%)
    pallas_call x1, Pallas kernels, per_device(): pl.pallas_call(functools.partial(kernel, bands, dirs, group), out_shape=(...  27.5 us
    pallas_call x1, Pallas kernels, per_device(): pl.pallas_call(put_out, out_shape=tuple((jax.ShapeDtypeStruct(x.shape, x....  0.7 us

profile of v2, /device:TPU:0, one launch (start us, length us, event | category | flops | bytes accessed | tf_op | source)
XLA Modules:
  0.0 28.9 jit_solution(4504535893808129474)
XLA Ops:
  0.6 27.5 %shard_map.67 = (f32[2,8,2,256]{3,2,1,0:T(2,128)S(1)}, f32[9,8,2,256]{3,2,1,0:T(2,128)S(1)}, f32[2,2]{1,0:T(2,128)S(1)}) custom-call(bf16[2,8,2,256,256]{4,3,2,1,0:T(8,128)(2,1)} %vis_hbm.1, bf16[2,8,2,256,256]{4,3,2,1,0:T(8,128)(2,1)} %sky_hbm.1, s32[2,8,8]{2,1,0:T(8,128)} %flags_hbm.1, s32[2]{0:T(128)} %dest_hbm.1), custom_call_target="tpu_custom_call" | custom-call | tf_op jit(solution)/shard_map/pallas_call | solution.py:550
  28.1 0.7 %shard_map.68 = (f32[2,8,2,256]{3,2,1,0:T(2,128)}, f32[9,8,2,256]{3,2,1,0:T(2,128)}, f32[2,2]{1,0:T(2,128)}) custom-call(f32[2,8,2,256]{3,2,1,0:T(2,128)S(1)} %get-tuple-element.6.refs_0_, f32[9,8,2,256]{3,2,1,0:T(2,128)S(1)} %get-tuple-element.7.refs_1_, f32[2,2]{1,0:T(2,128)S(1)} %get-tuple-element.8.refs_2_), custom_call_target="tpu_custom_call" | custom-call | tf_op jit(solution)/shard_map/pallas_call | solution.py:598

commit v3 on v2

--- a/solution.py
+++ b/solution.py
@@ -16,6 +16,10 @@
 LANES = 128
 TILE = 8
 PLAN = (("exact", "lead", "both", "held"), ("held", "held", "both", "held"))
+
+XLU = (2, 3)
+WAIT_STEPS = 5
+SPLIT = 2
 
 penalty_share = 0.4
 f32 = jnp.float32
@@ -59,6 +63,7 @@
     rest_num,
     rest_den,
     turned,
+    turned_low,
     keep,
     wpen,
     meta,
@@ -136,8 +141,9 @@
 
     for copy in small:
         copy.wait()
-    for copy in load(1) if chunks > 1 else ():
-        copy.start()
+    for c in range(1, min(3, chunks)):
+        for copy in load(c):
+            copy.start()
     row = row_of(tile)
     odd = lax.rem(row, 2) == 1
     sub_row = row // (2 * group)
@@ -155,13 +161,13 @@
         lane = row_of((1, stations), 1) // BLOCK
         for i in range(blocks):
             shape = (BLOCK, stations)
-            across = jnp.zeros((1, stations), f32)
+            line = jnp.zeros((1, stations), f32)
             for j in range(blocks):
-                across = jnp.where(lane == j, kept[j : j + 1, i : i + 1], across)
+                line = jnp.where(lane == j, kept[i : i + 1, j : j + 1], line)
             apart = row_of(shape) + i * BLOCK != row_of(shape, 1)
             keep[s, i * BLOCK : (i + 1) * BLOCK, :] = jnp.where(
-                apart, spread(across, shape), 0.0
-            )
+                apart, spread(line, shape), 0.0
+            ).astype(bf16)
     wpen[...] = penalty
     meta[me] = jnp.zeros(meta.shape[1:], f32)
     for s in range(subs):
@@ -237,30 +243,30 @@
         pen = wpen[...]
         return (num + pen * target) / (den + pen)
 
+    def turn(c, j):
+        s, k = j // group, j % group
+        for n in range(4):
+            value = vis[c, s, k, n] if n < 2 else sky[c, s, k, n - 2] * keep[s]
+            if n in XLU:
+                turned_low[j, n] = value.T
+            else:
+                turned[j, n] = lax.dot_general(
+                    identity, value, (((1,), (1,)), ((), ())), preferred_element_type=f32
+                )
+
     def build(c, out):
         num = jnp.zeros(tile, f32)
         den = jnp.zeros(tile, f32)
-
-        def turn(j):
-            for part, source in enumerate((vis, sky)):
-                for i in range(2):
-                    turned[j, 2 * part + i] = lax.dot_general(
-                        identity,
-                        source[c, j // group, j % group, i],
-                        (((1,), (1,)), ((), ())),
-                        preferred_element_type=f32,
-                    )
-
-        def fill(j, num, den):
-            s = j // group
+        if c < 3:
+            turn(c, 0)
+        for j in range(pairs):
             sums = [jnp.zeros((TILE, stations), f32) for _ in range(3)]
             for i in range(stations // BLOCK):
                 part = slice(i * BLOCK, (i + 1) * BLOCK)
-                baseline = keep[s, part, :]
-                data_re = turned[j, 0, part, :]
-                data_im = turned[j, 1, part, :]
-                model_re = baseline * turned[j, 2, part, :]
-                model_im = baseline * turned[j, 3, part, :]
+                data_re, data_im, model_re, model_im = (
+                    turned_low[j, n, part, :].astype(f32) if n in XLU else turned[j, n, part, :]
+                    for n in range(4)
+                )
                 values = (
                     model_re * data_re + model_im * data_im,
                     model_re * data_im - model_im * data_re,
@@ -279,15 +285,15 @@
                         base = j * stations + i * BLOCK
                         lead_den[c, base : base + BLOCK, :] = lead
                         rest_den[c, base : base + BLOCK, :] = rest
+                if i == 0:
+                    if j + 1 < pairs:
+                        turn(c, j + 1)
+                    elif 1 < c < chunks - 1:
+                        turn(c + 1, 0)
+                yield
             re, im, mag = (spread(jnp.sum(x, axis=0, keepdims=True), tile) for x in sums)
             num = jnp.where(row == 2 * j, re, jnp.where(row == 2 * j + 1, im, num))
             den = jnp.where(row // 2 == j, mag, den)
-            return num, den
-
-        for j in range(pairs):
-            turn(j)
-            num, den = fill(j, num, den)
-            yield
         out[c] = solved(num, den, ones)
 
     def sweeps(it, c, gain, out):
@@ -297,20 +303,42 @@
             if mode == "exact":
                 continue
             left_num, left_den = left_sides(gain)
-            num = times(left_num, lead_num[c])
-            den = times(left_den, lead_den[c])
+            step = stations * SPLIT
+            products = {}
+            for part, at_num, at_den in (
+                ("lead", lead_num, lead_den),
+                ("rest", rest_num, rest_den),
+            ):
+                if part == "rest" and mode != "both":
+                    continue
+                for j in range(0, pairs, SPLIT):
+                    at = slice(j * stations, j * stations + step)
+                    two = slice(2 * at.start, 2 * at.stop)
+                    got = (
+                        times(left_num[:, two], at_num[c, two, :]),
+                        times(left_den[:, at], at_den[c, at, :]),
+                    )
+                    if part in products:
+                        got = tuple(a + b for a, b in zip(products[part], got))
+                    products[part] = got
+                    yield False
+            num, den = products["lead"]
             if mode == "both":
-                low_num = times(left_num, rest_num[c])
-                low_den = times(left_den, rest_den[c])
+                low_num, low_den = products["rest"]
                 held[c, 0] = low_num
                 held[c, 1] = low_den
                 num, den = num + low_num, den + low_den
-            yield
+            yield True
             if mode == "held":
                 num, den = num + held[c, 0], den + held[c, 1]
             updated = solved(num, den, target)
             gain = 0.5 * (updated + gain) if index % 2 == 1 else updated
         out[c] = gain
+
+    def coarse(steps):
+        for ended in steps:
+            if ended:
+                yield
 
     def together(*steps):
         steps = list(steps)
@@ -320,6 +348,13 @@
                     next(step)
                 except StopIteration:
                     steps.remove(step)
+
+    def weave(main, side):
+        for ended in main:
+            for _ in range(WAIT_STEPS if ended else SPLIT):
+                next(side, None)
+        for _ in side:
+            pass
 
     def send(it, c, gain):
         gains[it, c, me] = gain
@@ -445,23 +480,27 @@
 
     first, after = {}, {}
     for c in range(chunks):
-        for copy in load(c):
-            copy.wait()
-        for n in range(max(2, c + 2), chunks if c == 0 else 0):
+        if c < 3:
+            for copy in load(c):
+                copy.wait()
+        for n in range(3, chunks if c == 0 else 0):
             for copy in load(n):
                 copy.start()
+        if 1 < c < chunks - 1:
+            for copy in load(c + 1):
+                copy.wait()
         if c == 1:
             pl.semaphore_wait(barrier, bands - 1 + dirs - 1)
             for peer in peers:
                 meta_copy(me, peer).start()
-        steps = [build(c, first)]
-        if c > 0:
-            steps.insert(0, sweeps(0, c - 1, first[c - 1], after))
-        together(*steps)
+        if c == 0:
+            together(build(c, first))
+        else:
+            weave(sweeps(0, c - 1, first[c - 1], after), build(c, first))
         if c > 0:
             send(0, c - 1, after[c - 1])
     all_of(meta.at[pl.ds(0, bands - 1)], meta_recv).wait()
-    together(solve(after), sweeps(0, chunks - 1, first[chunks - 1], after))
+    together(solve(after), coarse(sweeps(0, chunks - 1, first[chunks - 1], after)))
     send(0, chunks - 1, after[chunks - 1])
     weight_sum = after["weights"]
 
@@ -470,10 +509,27 @@
     pace = 2 if chunks % 2 == 0 else 1
     for base in range(0, chunks, pace):
         here = range(base, base + pace)
+        if pace == 2 and base + pace == chunks:
+            runs = []
+            for c in here:
+                arrive(0, c)
+                totals[0] = consensus(0, c, totals[0])
+                runs.append(coarse(sweeps(1, c, gains[0, c, me], after)))
+                if c == base:
+                    next(runs[0])
+                    next(runs[0])
+            for _ in range(2):
+                next(runs[0])
+                next(runs[1])
+            for c, run in zip(here, runs):
+                for _ in run:
+                    pass
+                send(1, c, after[c])
+            continue
         for c in here:
             arrive(0, c)
             totals[0] = consensus(0, c, totals[0])
-        together(*(sweeps(1, c, gains[0, c, me], after) for c in here))
+        together(*(coarse(sweeps(1, c, gains[0, c, me], after)) for c in here))
         for c in here:
             send(1, c, after[c])
 
@@ -566,7 +622,8 @@
             pltpu.VMEM((chunks, 2 * pairs * stations, stations), bf16),
             pltpu.VMEM((chunks, pairs * stations, stations), bf16),
             pltpu.VMEM((pairs, 4, stations, stations), f32),
-            pltpu.VMEM((subs, stations, stations), f32),
+            pltpu.VMEM((pairs, 4, stations, stations), bf16),
+            pltpu.VMEM((subs, stations, stations), bf16),
             pltpu.VMEM((rows, stations), f32),
             pltpu.VMEM((bands, meta_rows, width), f32),
             pltpu.VMEM((ITERS, chunks, bands, rows, stations), f32),

time: 29.1 us -> 27.6 us (0.948)
  Pallas kernels: 28.2 us -> 26.7 us
    pallas_call x1, Pallas kernels: 27.5 us -> 26 us  [per_device(): pl.pallas_call(functools.partial(kernel, bands, dirs, group), out_shape=(...]
where the time goes in v3:
time: 27.6 us; the launch traced here: 27.4 us
  Pallas kernels  26.7 us (97%)
  between operations  0.64 us (2%)
    pallas_call x1, Pallas kernels, per_device(): pl.pallas_call(functools.partial(kernel, bands, dirs, group), out_shape=(...  26 us
    pallas_call x1, Pallas kernels, per_device(): pl.pallas_call(put_out, out_shape=tuple((jax.ShapeDtypeStruct(x.shape, x....  0.7 us

profile of v3, /device:TPU:0, one launch (start us, length us, event | category | flops | bytes accessed | tf_op | source)
XLA Modules:
  0.0 27.4 jit_solution(1547179117455669234)
XLA Ops:
  0.6 26.0 %shard_map.67 = (f32[2,8,2,256]{3,2,1,0:T(2,128)S(1)}, f32[9,8,2,256]{3,2,1,0:T(2,128)S(1)}, f32[2,2]{1,0:T(2,128)S(1)}) custom-call(bf16[2,8,2,256,256]{4,3,2,1,0:T(8,128)(2,1)} %vis_hbm.1, bf16[2,8,2,256,256]{4,3,2,1,0:T(8,128)(2,1)} %sky_hbm.1, s32[2,8,8]{2,1,0:T(8,128)} %flags_hbm.1, s32[2]{0:T(128)} %dest_hbm.1), custom_call_target="tpu_custom_call" | custom-call | tf_op jit(solution)/shard_map/pallas_call | solution.py:606
  26.7 0.7 %shard_map.68 = (f32[2,8,2,256]{3,2,1,0:T(2,128)}, f32[9,8,2,256]{3,2,1,0:T(2,128)}, f32[2,2]{1,0:T(2,128)}) custom-call(f32[2,8,2,256]{3,2,1,0:T(2,128)S(1)} %get-tuple-element.6.refs_0_, f32[9,8,2,256]{3,2,1,0:T(2,128)S(1)} %get-tuple-element.7.refs_1_, f32[2,2]{1,0:T(2,128)S(1)} %get-tuple-element.8.refs_2_), custom_call_target="tpu_custom_call" | custom-call | tf_op jit(solution)/shard_map/pallas_call | solution.py:655
